TPU v7x, 32 devices: a whole 2x2x4 slice. The times are simulated.
32 devices in a mesh: seq: 8 (over z, y), head: 4 (over x, core).
Axes of the slice: x: 2, y: 2, z: 4, core: 2. Of those that a mesh axis runs over, the one named last changes fastest.
Arguments:
- hidden_states: bfloat16 [8, 512, 3584], P(None, 'seq', 'head'), may hold values from -6 to 6
- boundary: int32 [8, 64], replicated, may hold values from 0 to 511, as said below
- valid: int32 [8, 64], replicated, may hold values from 0 to 1, as said below
- pairs: int32 [8, 2], replicated, may hold values from 0 to 7, as said below
- w_first: bfloat16 [3584, 4096], P('seq', 'head'), may hold values from -0.09375 to 0.09375
- b_first: float32 [4096], P('head'), may hold values from -3 to 3
- w_second: float32 [4096], P('head'), may hold values from -0.09375 to 0.09375
Outputs:
- step_reward: float32 [8, 64], replicated
- trace_score: float32 [8], replicated
- margin: float32 [8], replicated
Inputs may be any that keep to these rules, and one draw needn't show every extreme that they name: Within a trace the 64 boundary positions are distinct and increasing. In each trace the ones come first; every trace has 16 to 64 valid steps. `pairs`: the two traces of a pair differ.
All inputs are finite; a program needn't handle non-finite values.
Results may differ from a plain program's by a relative error of at most 0.0003.
Values may be sent and summed in bfloat16 or wider, within the bound.
A program may use at most 64 MiB of HBM per device.

v0:
```python
import functools

import jax
import jax.numpy as jnp
from jax import lax
from jax.experimental import pallas as pl
from jax.experimental.pallas import tpu as pltpu
from jax.sharding import PartitionSpec as P

MESH = pl.DeviceIdType.MESH


def score_rows(rows, w_first, b_first, w_second):
    pre = jnp.dot(
        rows, lax.all_gather(w_first, "seq", axis=0, tiled=True), preferred_element_type=jnp.float32
    )
    return jnp.sum(jnp.maximum(pre + b_first, 0.0) * w_second, axis=-1)


def per_device(hidden_states, boundary, valid, pairs, w_first, b_first, w_second):
    traces, tok_dev, quarter = hidden_states.shape
    offset = lax.axis_index("seq") * tok_dev
    positions = offset + jnp.arange(tok_dev, dtype=jnp.int32)
    hits = boundary[:, :, None] == positions[None, None, :]
    whole = lax.all_gather(hidden_states, "head", axis=2, tiled=True)
    token_logit = score_rows(
        whole.reshape(traces * tok_dev, whole.shape[2]), w_first, b_first, w_second
    )
    token_logit = token_logit.reshape(traces, tok_dev)
    partial_logit = jnp.sum(jnp.where(hits, token_logit[:, None, :], 0.0), axis=2)
    logit = lax.psum(partial_logit, ("seq", "head"))
    live = valid == 1
    step_reward = jnp.where(live, logit, jnp.float32(0.0))
    trace_score = jnp.min(jnp.where(live, logit, jnp.float32(1e30)), axis=1)
    trace_ids = jnp.arange(traces, dtype=jnp.int32)[None, :]
    winner = jnp.sum(jnp.where(pairs[:, 0:1] == trace_ids, trace_score[None, :], 0.0), axis=1)
    loser = jnp.sum(jnp.where(pairs[:, 1:2] == trace_ids, trace_score[None, :], 0.0), axis=1)
    return (step_reward, trace_score, winner - loser)


def kernel(
    n_seq, n_head, hid_hbm, bnd, valid, pairs, w_hbm, b, w2, reward, score, margin,
    hid, w, s_hid, s_win,
    xout, xin, xacc, xup, xdn, xall, wown, wall, psend, precv, fsend, frecv,
    s_x1, r_x1, s_w, r_w, s_x2, r_up, r_dn, s_x3, r_x3, s_p, r_p, s_f, r_f,
):
    fetch_hid = pltpu.make_async_copy(hid_hbm, hid, s_hid)
    fetch_w = pltpu.make_async_copy(w_hbm, w, s_win)
    fetch_hid.start()
    fetch_w.start()
    traces, toks, _ = hid.shape
    half = traces
    block = bnd.shape[1] // 2
    planes = n_seq // 2
    depth = w.shape[0]
    cols = w.shape[1] // 2
    s = lax.axis_index("seq")
    h = lax.axis_index("head")
    z = s // 2
    y = s % 2
    other = 1 - y

    def remote(src, dst, send, recv, to_s, to_h):
        return pltpu.make_async_remote_copy(
            src_ref=src, dst_ref=dst, send_sem=send, recv_sem=recv,
            device_id=(to_s, to_h), device_id_type=MESH,
        )

    across = s + 1 - 2 * y
    h_core = h + 1 - 2 * (h % 2)
    h_x = lax.rem(h + 2, n_head)

    barrier = pltpu.get_barrier_semaphore()

    def greet(to_s, to_h):
        pl.semaphore_signal(barrier, inc=1, device_id=(to_s, to_h), device_id_type=MESH)

    greet(across, h)
    greet(s, h_core)
    greet(s, h_x)

    @pl.when(z > 0)
    def _():
        greet(s - 2, h)

    @pl.when(z < planes - 1)
    def _():
        greet(s + 2, h)

    def pick(t):
        pos = lax.broadcasted_iota(jnp.int32, (toks, bnd.shape[1]), 0) + s * toks
        hot = jnp.where(bnd[pl.ds(t, 1), :] == pos, 1.0, 0.0).astype(jnp.bfloat16)
        got = lax.dot_general(
            hot, hid[t], (((0,), (0,)), ((), ())), preferred_element_type=jnp.float32
        )
        return got.astype(jnp.bfloat16)

    def copy_x1(k):
        return remote(xout.at[k], xin.at[k], s_x1.at[k], r_x1.at[k], across, h)

    def my_cols(which):
        return pl.ds(pl.multiple_of(which * cols, cols), cols)

    part = depth // 2

    def copy_w(i):
        rows = pl.ds(pl.multiple_of(y * depth + i * part, part), part)
        return remote(wown.at[pl.ds(i * part, part)], wall.at[rows], s_w.at[i], r_w.at[i], across, h)

    def pick_half(which, dst):
        for i in range(traces // 2):
            got = pick(which * (traces // 2) + i)
            dst[2 * i] = got[:block]
            dst[2 * i + 1] = got[block:]

    fetch_hid.wait()
    pick_half(other, xout)
    pl.semaphore_wait(
        barrier, 3 + jnp.where(z > 0, 1, 0) + jnp.where(z < planes - 1, 1, 0)
    )
    for k in range(half):
        copy_x1(k).start()
    fetch_w.wait()
    wown[...] = w[:, my_cols(other)]
    for i in range(2):
        copy_w(i).start()
    wall[pl.ds(pl.multiple_of(y * depth, depth), depth), :] = w[:, my_cols(y)]

    pick_half(y, xacc)

    same_core = (h % 2) == (z % 2)

    def copy_x3(t, way):
        to_s, to_h = ((s, h_core), (across, h), (s, h_x))[way]
        return remote(xall.at[t], xall.at[t], s_x3.at[t, way], r_x3.at[t], to_s, to_h)

    is_root = z == h
    from_up = (z >= h) & (z < planes - 1)
    from_dn = (z <= h) & (z > 0)

    def copy_down(k):
        return remote(xacc.at[k], xup.at[k], s_x2.at[k], r_up.at[k], lax.rem(s + n_seq - 2, n_seq), h)

    def copy_up(k):
        return remote(xacc.at[k], xdn.at[k], s_x2.at[k], r_dn.at[k], lax.rem(s + 2, n_seq), h)

    def chain(k):
        copy_x1(k).wait_recv()
        xacc[k] = xacc[k] + xin[k]

        @pl.when(from_up)
        def _():
            copy_down(k).wait_recv()
            xacc[k] = xacc[k] + xup[k]

        @pl.when(from_dn)
        def _():
            copy_up(k).wait_recv()
            xacc[k] = xacc[k] + xdn[k]

        @pl.when(z > h)
        def _():
            copy_down(k).start()

        @pl.when(z < h)
        def _():
            copy_up(k).start()

        @pl.when(is_root)
        def _():
            t = y * half + k
            xall[t] = xacc[k]
            copy_x3(t, 1).start()
            copy_x3(t, 2).start()
            copy_x3(t, 0).start()

    def spread(k):
        t = y * half + k

        @pl.when(jnp.logical_not(is_root))
        def _():
            copy_x3(t, 0).wait_recv()

            @pl.when(same_core)
            def _():
                copy_x3(t, 1).start()
                copy_x3(t, 0).start()

    def spread_far(k):
        t = other * half + k
        copy_x3(t, 0).wait_recv()

        @pl.when(same_core)
        def _():
            copy_x3(t, 0).start()

    for k in range(half):
        chain(k)
    def copy_p(t, down):
        to_s = lax.rem(s + n_seq - 2, n_seq) if down else lax.rem(s + 2, n_seq)
        return remote(psend.at[t], precv.at[t], s_p.at[t], r_p.at[t], to_s, h)

    bias = b[:, my_cols(y)]
    out_row = w2[:, my_cols(y)]
    lanes = lax.broadcasted_iota(jnp.int32, (block, 128), 1)
    fsend[...] = jnp.zeros_like(fsend)

    lag = 3

    def reduce_step(tick):
        for down in (True, False):
            first = planes - 1 if down else 0
            last = planes - 1 - first
            k = tick - lag * (planes - 1 - z if down else z)
            t = k if down else half + k

            @pl.when((k >= 0) & (k < half))
            def _():
                psend[t] = jnp.dot(xall[t], wall[...], preferred_element_type=jnp.float32)

                @pl.when(z != first)
                def _():
                    copy_p(t, down).wait_recv()
                    psend[t] = psend[t] + precv[t]

                @pl.when(z != last)
                def _():
                    copy_p(t, down).start()

                @pl.when(z == last)
                def _():
                    act = jnp.maximum(psend[t] + bias, 0.0) * out_row
                    total = jnp.sum(act, axis=1, keepdims=True)
                    here = pl.ds(pl.multiple_of((k % 2) * block, block), block)
                    fsend[here, :] = fsend[here, :] + jnp.where(lanes == k // 2, total, 0.0)

    for k in range(half):
        spread(k)
    for k in range(half):
        spread_far(k)
        if k == 0:
            for i in range(2):
                copy_w(i).wait_recv()
        reduce_step(k)
    for k in range(half, half + lag * (planes - 1)):
        reduce_step(k)

    is_end = (z == 0) | (z == planes - 1)
    slots = 4 * n_head
    me = s * n_head + h
    n_dev = n_seq * n_head
    slot = jnp.where(z == 0, 0, 1) * (2 * n_head) + y * n_head + h

    def copy_f(d):
        to = lax.rem(me + d, n_dev)
        return remote(
            frecv.at[slot], frecv.at[slot], s_f.at[d], r_f.at[slot], to // n_head, lax.rem(to, n_head)
        )

    @pl.when(is_end)
    def _():
        frecv[slot] = jnp.transpose(fsend[...])[: frecv.shape[1], :]
        for d in range(1, n_dev):
            copy_f(d).start()

    sums = [jnp.zeros(frecv.shape[1:], jnp.float32) for _ in range(2)]
    for i in range(slots):

        @pl.when(jnp.logical_not(is_end & (slot == i)))
        def _():
            remote(frecv.at[i], frecv.at[i], s_f.at[0], r_f.at[i], across, h).wait_recv()

        side = i // (2 * n_head)
        sums[side] = sums[side] + frecv[i]

    logit = jnp.concatenate(sums, axis=0)

    live = valid[...] == 1
    reward[...] = jnp.where(live, logit, 0.0)
    low = jnp.min(jnp.where(live, logit, 1e30), axis=1, keepdims=True)
    square = (traces, traces)
    eye = lax.broadcasted_iota(jnp.int32, square, 0) == lax.broadcasted_iota(jnp.int32, square, 1)
    score[...] = jnp.sum(jnp.where(eye, low, 0.0), axis=0)
    ids = lax.broadcasted_iota(jnp.int32, (traces, pairs.shape[1]), 0)
    winner = jnp.sum(jnp.where(pairs[0:1, :] == ids, low, 0.0), axis=0)
    loser = jnp.sum(jnp.where(pairs[1:2, :] == ids, low, 0.0), axis=0)
    margin[...] = winner - loser

    for i in range(2):
        copy_w(i).wait_send()
    for k in range(half):
        copy_x1(k).wait_send()

        @pl.when(jnp.logical_not(is_root))
        def _():
            copy_down(k).wait_send()

        for t, near in ((y * half + k, True), (other * half + k, False)):

            @pl.when(same_core)
            def _():
                copy_x3(t, 0).wait_send()
                if near:
                    copy_x3(t, 1).wait_send()

        @pl.when(is_root)
        def _():
            copy_x3(y * half + k, 2).wait_send()

        @pl.when(z != 0)
        def _():
            copy_p(k, True).wait_send()

        @pl.when(z != planes - 1)
        def _():
            copy_p(half + k, False).wait_send()

    @pl.when(is_end)
    def _():
        for d in range(1, n_dev):
            copy_f(d).wait_send()


def fused(n_seq, n_head, hidden_states, boundary, valid, pairs, w_first, b_first, w_second):
    traces, toks, feats = hidden_states.shape
    steps = boundary.shape[1]
    depth, width = w_first.shape
    half, block, cols = traces, steps // 2, width // 2
    bf16, f32 = jnp.bfloat16, jnp.float32
    dma = pltpu.SemaphoreType.DMA
    vmem = pl.BlockSpec(memory_space=pltpu.VMEM)
    hbm = pl.BlockSpec(memory_space=pl.ANY)
    return pl.pallas_call(
        functools.partial(kernel, n_seq, n_head),
        out_shape=(
            jax.ShapeDtypeStruct((traces, steps), f32),
            jax.ShapeDtypeStruct((traces,), f32),
            jax.ShapeDtypeStruct((pairs.shape[0],), f32),
        ),
        in_specs=[hbm] + [vmem] * 3 + [hbm] + [vmem] * 2,
        out_specs=(vmem,) * 3,
        scratch_shapes=[
            pltpu.VMEM((traces, toks, feats), bf16),
            pltpu.VMEM((depth, width), bf16),
            dma, dma,
            pltpu.VMEM((half, block, feats), bf16),
            pltpu.VMEM((half, block, feats), bf16),
            pltpu.VMEM((half, block, feats), bf16),
            pltpu.VMEM((half, block, feats), bf16),
            pltpu.VMEM((half, block, feats), bf16),
            pltpu.VMEM((2 * half, block, feats), bf16),
            pltpu.VMEM((depth, cols), bf16),
            pltpu.VMEM((2 * depth, cols), bf16),
            pltpu.VMEM((2 * half, block, cols), f32),
            pltpu.VMEM((2 * half, block, cols), f32),
            pltpu.VMEM((steps, 128), f32),
            pltpu.VMEM((4 * n_head, traces // 2, steps), f32),
            dma((half,)), dma((half,)),
            dma((2,)), dma((2,)),
            dma((half,)), dma((half,)), dma((half,)),
            dma((2 * half, 3)), dma((2 * half,)),
            dma((2 * half,)), dma((2 * half,)),
            dma((n_seq * n_head,)), dma((4 * n_head,)),
        ],
        compiler_params=pltpu.CompilerParams(collective_id=0, has_side_effects=True),
    )(
        hidden_states, boundary, valid, pairs.T, w_first,
        b_first.reshape(1, width), w_second.reshape(1, width),
    )


def solution(mesh):
    n_seq, n_head = mesh.shape["seq"], mesh.shape["head"]
    paired = n_seq == 2 * n_head and n_head % 4 == 0
    body = functools.partial(fused, n_seq, n_head) if paired else per_device
    placed = (P(None, "seq", "head"), P(), P(), P(), P("seq", "head"), P("head"), P("head"))
    return jax.shard_map(
        body, mesh=mesh, in_specs=placed, out_specs=(P(), P(), P()), check_vma=False
    )
```

profile of v0, /device:TPU:0, one launch (start us, length us, event | category | flops | bytes accessed | tf_op | source)
XLA Modules:
  0.0 62.1 jit_solution(18309410453814387260)
XLA Ops:
  0.6 59.1 %shard_map.94 = (f32[8,64]{1,0:T(8,128)}, f32[8]{0:T(128)}, f32[8]{0:T(128)}) custom-call(bf16[8,64,896]{2,1,0:T(8,128)(2,1)} %hid_hbm.1, s32[8,64]{1,0:T(8,128)} %bnd.1, s32[8,64]{1,0:T(8,128)} %valid.1, s32[2,8]{1,0:T(2,128)} %bitcast.5, bf16[448,1024]{1,0:T(8,128)(2,1)} %w_hbm.1, f32[1,1024]{1,0:T(1,128)} %bitcast.3, f32[1,1024]{1,0:T(1,128)} %bitcast.4), custom_call_target="tpu_custom_call" | custom-call | tf_op jit(solution)/shard_map/pallas_call | solution.py:333
  59.7 0.0 copy-start
  59.7 0.7 %copy-done = f32[8,64]{1,0:T(8,128)S(1)} copy-done((f32[8,64]{1,0:T(8,128)S(1)}, f32[8,64]{1,0:T(8,128)}, u32[]{:S(2)}) %copy-start) | copy-done | bytes 2072
  60.4 0.0 copy-start.2
  60.4 0.6 copy.13
  61.0 0.0 copy-done.2
  61.0 0.0 copy-start.1
  61.0 0.5 copy.14
  61.5 0.1 copy-done.1
  61.6 0.5 copy.15
Async XLA Ops:
  59.7 0.7 %copy-start = (f32[8,64]{1,0:T(8,128)S(1)}, f32[8,64]{1,0:T(8,128)}, u32[]{:S(2)}) copy-start(f32[8,64]{1,0:T(8,128)} %get-tuple-element.6) | copy-start | bytes 6148
  60.4 0.6 copy-start.2
  61.0 0.6 copy-start.1
where the time goes:
time: 62.4 us; the launch traced here: 62.1 us
  Pallas kernels  59.1 us (95%)
  local copies, waits for them, and re-layouts  2.38 us (4%)
  between operations  0.65 us (1%)
    pallas_call x1, Pallas kernels, fused(): pl.pallas_call(functools.partial(kernel, n_seq, n_head), out_shape=(jax.S...  59.1 us
    unnamed x9, local copies, waits for them, and re-layouts  2.38 us

commit v1 on v0

v1 whole, which is shorter than its diff:
```python
import functools

import jax
import jax.numpy as jnp
from jax import lax
from jax.experimental import pallas as pl
from jax.experimental.pallas import tpu as pltpu
from jax.sharding import PartitionSpec as P

MESH = pl.DeviceIdType.MESH
SPAN = 128
HUB_FIRST = 0
EARLY = 1
W_MEMBER = (-8, -6, -4, -1)
W_OUTER = (-8, 7, 7, 7)
W_MIDDLE = (-8, -6, -4, -1)
PARTS = 1
AHEAD = 1
LAG_Y = 8
LAG_Z = 16


def schedule(blocks, chunks):
    order = [(k, c) for k in range(blocks) for c in range(chunks)]
    left = {k: chunks for k in range(blocks)}
    ops, pending, got = [], [], 0
    for i in range(len(order) + LAG_Y):
        if i < len(order):
            k, c = order[i]
            while got < min(blocks, k + 1 + AHEAD):
                ops.append((0, got, 0))
                got += 1
            if c == 0:
                ops.append((1, k, 0))
            ops.append((2, k, c))
        if i >= LAG_Y:
            k, c = order[i - LAG_Y]
            ops.append((3, k, c))
            left[k] -= 1
            if left[k] == 0:
                pending.append((i + LAG_Z, k))
        while pending and pending[0][0] <= i:
            ops.append((4, pending.pop(0)[1], 0))
    return ops + [(4, k, 0) for _, k in pending]


def score_rows(rows, w_first, b_first, w_second):
    pre = jnp.dot(
        rows, lax.all_gather(w_first, "seq", axis=0, tiled=True), preferred_element_type=jnp.float32
    )
    return jnp.sum(jnp.maximum(pre + b_first, 0.0) * w_second, axis=-1)


def per_device(hidden_states, boundary, valid, pairs, w_first, b_first, w_second):
    traces, tok_dev, quarter = hidden_states.shape
    offset = lax.axis_index("seq") * tok_dev
    positions = offset + jnp.arange(tok_dev, dtype=jnp.int32)
    hits = boundary[:, :, None] == positions[None, None, :]
    whole = lax.all_gather(hidden_states, "head", axis=2, tiled=True)
    token_logit = score_rows(
        whole.reshape(traces * tok_dev, whole.shape[2]), w_first, b_first, w_second
    )
    token_logit = token_logit.reshape(traces, tok_dev)
    partial_logit = jnp.sum(jnp.where(hits, token_logit[:, None, :], 0.0), axis=2)
    logit = lax.psum(partial_logit, ("seq", "head"))
    live = valid == 1
    step_reward = jnp.where(live, logit, jnp.float32(0.0))
    trace_score = jnp.min(jnp.where(live, logit, jnp.float32(1e30)), axis=1)
    trace_ids = jnp.arange(traces, dtype=jnp.int32)[None, :]
    winner = jnp.sum(jnp.where(pairs[:, 0:1] == trace_ids, trace_score[None, :], 0.0), axis=1)
    loser = jnp.sum(jnp.where(pairs[:, 1:2] == trace_ids, trace_score[None, :], 0.0), axis=1)
    return (step_reward, trace_score, winner - loser)


def kernel(
    n_seq, n_head, hid_hbm, bnd, valid, pairs, w_hbm, b, w2, result,
    hid, xo, xin, xup, xdn, xq, xl, wown, wall,
    ysend, yrecv, zsend, zrecv, kept, fsend, frecv, far,
    s_hid, s_win, s_x1, r_x1, s_w, r_w, s_x2, r_up, r_dn, s_x3, r_x3,
    s_y, r_y, s_z, r_z, s_f, r_f,
):
    traces, toks, feats = hid.shape
    blocks, block, _ = xin.shape
    steps = bnd.shape[1]
    planes = n_seq // 2
    depth = w_hbm.shape[0]
    cols = w_hbm.shape[1] // 2
    chunks, _, span = wown.shape
    groups = traces // 2
    s = lax.axis_index("seq")
    h = lax.axis_index("head")
    z = s // 2
    y = s % 2
    other = 1 - y
    odd = z % 2
    high = z // 2
    par = h % 2
    lanes = lax.broadcasted_iota(jnp.int32, (block, feats), 1)

    def fetch_w(c, mine):
        first = pl.multiple_of((odd if mine else 1 - odd) * cols + c * span, span)
        rows = pl.ds(pl.multiple_of(odd * depth, depth), depth)
        return pltpu.make_async_copy(
            w_hbm.at[:, pl.ds(first, span)],
            wall.at[c, rows, :] if mine else wown.at[c],
            s_win.at[c, 1 if mine else 0],
        )

    def trace_of(k):
        return (k % 2) * groups + k // 2

    def fetch_hid(k):
        t = trace_of(k)
        return pltpu.make_async_copy(hid_hbm.at[t], hid.at[t], s_hid.at[t])

    for k in range(blocks):
        fetch_hid(k).start()
        if k % 2 == 1 and k // 2 < chunks:
            fetch_w(k // 2, False).start()

    def remote(src, dst, send, recv, to_s, to_h):
        return pltpu.make_async_remote_copy(
            src_ref=src, dst_ref=dst, send_sem=send, recv_sem=recv,
            device_id=(to_s, to_h), device_id_type=MESH,
        )

    across = s + 1 - 2 * y
    h_core = h + 1 - 2 * par
    h_x = lax.rem(h + 2, n_head)
    s_near = s + 2 - 4 * odd
    s_far = lax.rem(s + n_seq // 2, n_seq)
    is_end = (z == 0) | (z == planes - 1)
    middle = jnp.logical_not(is_end)
    member = (h // 2) == high
    hub = member & middle

    barrier = pltpu.get_barrier_semaphore()

    def greet(to_s, to_h):
        pl.semaphore_signal(barrier, inc=1, device_id=(to_s, to_h), device_id_type=MESH)

    greet(across, h)
    greet(s, h_core)
    greet(s, h_x)

    @pl.when(z > 0)
    def _():
        greet(s - 2, h)

    @pl.when(z < planes - 1)
    def _():
        greet(s + 2, h)

    def turn(rows):
        return jnp.concatenate([rows[:, feats // 2 :], rows[:, : feats // 2]], axis=1)

    def fold(low, high_rows):
        return (
            jnp.where(lanes < feats // 2, low, turn(high_rows)),
            jnp.where(lanes < feats // 2, turn(low), high_rows),
        )

    def pick(k):
        t = trace_of(k)
        fetch_hid(k).wait()
        pos = lax.broadcasted_iota(jnp.int32, (toks, steps), 0) + s * toks
        hot = jnp.where(bnd[pl.ds(t, 1), :] == pos, 1.0, 0.0).astype(jnp.bfloat16)
        got = lax.dot_general(
            hot, hid[t], (((0,), (0,)), ((), ())), preferred_element_type=jnp.float32
        )
        pair = fold(got[:block], got[block:])
        for half in range(2):
            xo[half, k] = pair[half].astype(jnp.bfloat16)

    size = block // PARTS
    pieces = blocks * PARTS

    def rows_of(n):
        return pl.ds((n % PARTS) * size, size)

    def copy_x1(n):
        k, rows = n // PARTS, rows_of(n)
        return remote(
            xo.at[other, k, rows], xin.at[k, rows], s_x1.at[n], r_x1.at[n], across, h
        )

    def copy_w(c):
        rows = pl.ds(pl.multiple_of(odd * depth, depth), depth)
        return remote(wown.at[c], wall.at[c, rows, :], s_w.at[c], r_w.at[c], s_near, h)

    for k in range(EARLY):
        pick(k)
    pl.semaphore_wait(
        barrier, 3 + jnp.where(z > 0, 1, 0) + jnp.where(z < planes - 1, 1, 0)
    )
    def send_w(k):
        for c in range(chunks):
            for plan, who in (
                (W_MEMBER, member & is_end),
                (W_OUTER, jnp.logical_not(member) & is_end),
                (W_MIDDLE, middle),
            ):
                if plan[c] == k:

                    @pl.when(who)
                    def _():
                        fetch_w(c, False).wait()
                        copy_w(c).start()

    for k in range(blocks):
        if k >= EARLY:
            pick(k)
        for p in range(PARTS):
            copy_x1(k * PARTS + p).start()
        send_w(k - blocks)
    for c in range(chunks):
        fetch_w(c, True).start()

    @pl.when(middle)
    def _():
        pl.semaphore_signal(far, inc=1, device_id=(s - 2, h), device_id_type=MESH)
        pl.semaphore_signal(far, inc=1, device_id=(s + 2, h), device_id_type=MESH)

    def copy_up(n):
        k, rows = n // PARTS, rows_of(n)
        to_s = jnp.where(member, s_near, jnp.where(h >= n_head // 2, s + 2, s - 2))
        return remote(
            xo.at[y, k, rows], xup.at[k, rows], s_x2.at[n], r_up.at[n],
            lax.rem(to_s + n_seq, n_seq), h,
        )

    def copy_dn(n):
        k, rows = n // PARTS, rows_of(n)
        return remote(xo.at[y, k, rows], xdn.at[k, rows], s_x2.at[n], r_dn.at[n], s_near, h)

    def copy_x3(q, n, way):
        k, rows = n // PARTS, rows_of(n)
        to_h = h_x if way else h_core
        return remote(
            xq.at[q, k, rows], xq.at[q, k, rows], s_x3.at[way * pieces + n],
            r_x3.at[q * pieces + n], s, to_h,
        )

    def relay(n):
        k, rows = n // PARTS, rows_of(n)
        copy_x1(n).wait_recv()
        xo[y, k, rows] = xo[y, k, rows] + xin[k, rows]

        @pl.when(middle)
        def _():
            copy_up(n).wait_recv()
            xo[y, k, rows] = xo[y, k, rows] + xup[k, rows]

        @pl.when(member)
        def _():
            copy_dn(n).start()

        @pl.when(jnp.logical_not(member))
        def _():
            copy_up(n).start()

    def gather(n):
        k, rows = n // PARTS, rows_of(n)
        copy_x1(n).wait_recv()
        copy_up(n).wait_recv()
        xo[y, k, rows] = (xo[y, k, rows] + xin[k, rows]) + xup[k, rows]
        copy_up(n).start()
        copy_dn(n).wait_recv()
        xq[par, k, rows] = xo[y, k, rows] + xdn[k, rows]
        copy_x3(par, n, 1).start()
        copy_x3(par, n, 0).start()

    def collect(n):
        k, rows = n // PARTS, rows_of(n)
        if k >= HUB_FIRST:

            @pl.when(hub)
            def _():
                gather(n)

        @pl.when(member & is_end)
        def _():
            copy_up(n).wait_recv()
            xq[par, k, rows] = xo[y, k, rows] + xup[k, rows]
            copy_x3(par, n, 1).start()

        @pl.when(jnp.logical_not(member))
        def _():
            copy_x3(par, n, 1).wait_recv()

        @pl.when(jnp.logical_not(hub))
        def _():
            copy_x3(par, n, 0).start()

    def ready(k):
        for p in range(PARTS):
            copy_x3(1 - par, k * PARTS + p, 0).wait_recv()
        low = xq[0, k].astype(jnp.float32)
        top = xq[1, k].astype(jnp.float32)
        pair = fold(low, top)
        xl[k, :block] = pair[0].astype(jnp.bfloat16)
        xl[k, block:] = pair[1].astype(jnp.bfloat16)

    @pl.when(jnp.logical_not(hub))
    def _():
        for k in range(blocks):
            for p in range(PARTS):
                relay(k * PARTS + p)
            send_w(k)

    @pl.when(hub)
    def _():
        for n in range(HUB_FIRST * PARTS):
            gather(n)

    def copy_y(t):
        return remote(ysend.at[t], yrecv.at[t], s_y.at[t], r_y.at[t], across, h)

    def copy_z(t):
        return remote(zsend.at[t], zrecv.at[t], s_z.at[t], r_z.at[t], s_far, h)

    spots = lax.broadcasted_iota(jnp.int32, (steps, 128), 1)
    fsend[...] = jnp.zeros_like(fsend)

    def part(k, c):
        return jnp.dot(xl[k], wall[c], preferred_element_type=jnp.float32)

    def give(k, c):
        t = k * (chunks // 2) + c // 2

        @pl.when(c % 2 != y)
        def _():
            ysend[t] = part(k, c)
            copy_y(t).start()

    def take(k, c):
        t = k * (chunks // 2) + c // 2

        @pl.when((c % 2 == y) & (c // 2 != high))
        def _():
            zsend[k] = part(k, c)
            copy_y(t).wait_recv()
            zsend[k] = zsend[k] + yrecv[t]
            copy_z(k).start()

        @pl.when((c % 2 == y) & (c // 2 == high))
        def _():
            kept[k] = part(k, c)
            copy_y(t).wait_recv()
            kept[k] = kept[k] + yrecv[t]

    at = pl.ds(pl.multiple_of((odd * chunks + 2 * high + y) * span, span), span)
    bias = b[:, at]
    out_row = w2[:, at]

    def finish(k):
        copy_z(k).wait_recv()
        act = jnp.maximum(kept[k] + zrecv[k] + bias, 0.0) * out_row
        total = jnp.sum(act, axis=1, keepdims=True)
        fsend[...] = fsend[...] + jnp.where(spots == trace_of(k), total, 0.0)

    pl.semaphore_wait(far, 1)
    arrived = set()
    for kind, k, c in schedule(blocks, chunks):
        if kind == 0:
            for p in range(PARTS):
                collect(k * PARTS + p)
        elif kind == 1:
            ready(k)
        elif kind == 4:
            finish(k)
        else:
            if c not in arrived:
                arrived.add(c)
                fetch_w(c, True).wait()
                copy_w(c).wait_recv()
            (give if kind == 2 else take)(k, c)

    me = s * n_head + h
    n_dev = n_seq * n_head

    def copy_f(d):
        to = lax.rem(me + d, n_dev)
        return remote(
            frecv.at[me], frecv.at[me], s_f.at[d], r_f.at[me], to // n_head, lax.rem(to, n_head)
        )

    frecv[me] = jnp.transpose(fsend[...])[: frecv.shape[1], :]
    for d in range(1, n_dev):
        copy_f(d).start()
    for i in range(n_dev):

        @pl.when(me != i)
        def _():
            remote(frecv.at[i], frecv.at[i], s_f.at[0], r_f.at[i], across, h).wait_recv()

    sums = [frecv[i] for i in range(4)]
    for i in range(4, n_dev):
        sums[i % 4] = sums[i % 4] + frecv[i]
    logit = (sums[0] + sums[1]) + (sums[2] + sums[3])

    live = valid[...] == 1
    low = jnp.min(jnp.where(live, logit, 1e30), axis=1, keepdims=True)
    ids = lax.broadcasted_iota(jnp.int32, (traces, pairs.shape[1]), 0)
    square = (pairs.shape[1], pairs.shape[1])
    eye = lax.broadcasted_iota(jnp.int32, square, 0) == lax.broadcasted_iota(jnp.int32, square, 1)
    winner = jnp.sum(jnp.where(pairs[0:1, :] == ids, low, 0.0), axis=0, keepdims=True)
    loser = jnp.sum(jnp.where(pairs[1:2, :] == ids, low, 0.0), axis=0, keepdims=True)
    gap = jnp.sum(jnp.where(eye, winner - loser, 0.0), axis=1, keepdims=True)
    result[:traces, :steps] = jnp.where(live, logit, 0.0)
    result[:traces, steps : steps + 1] = low
    result[: pairs.shape[1], steps + 1 : steps + 2] = gap

    for c in range(chunks):
        copy_w(c).wait_send()
    for n in range(pieces):
        copy_x1(n).wait_send()
        copy_up(n).wait_send()
        copy_x3(par, n, 0).wait_send()

        @pl.when(member)
        def _():
            copy_x3(par, n, 1).wait_send()

    for t in range(blocks * chunks // 2):
        copy_y(t).wait_send()
    for k in range(blocks):
        copy_z(k).wait_send()
    for d in range(1, n_dev):
        copy_f(d).wait_send()


def fused(n_seq, n_head, hidden_states, boundary, valid, pairs, w_first, b_first, w_second):
    traces, toks, feats = hidden_states.shape
    steps = boundary.shape[1]
    depth, width = w_first.shape
    block, cols = steps // 2, width // 2
    chunks = cols // SPAN
    mine = traces * chunks // 2
    pieces = traces * PARTS
    n_dev = n_seq * n_head
    bf16, f32 = jnp.bfloat16, jnp.float32
    dma = pltpu.SemaphoreType.DMA
    vmem = pl.BlockSpec(memory_space=pltpu.VMEM)
    hbm = pl.BlockSpec(memory_space=pl.ANY)
    result = pl.pallas_call(
        functools.partial(kernel, n_seq, n_head),
        out_shape=jax.ShapeDtypeStruct((max(traces, pairs.shape[0]), steps + 64), f32),
        in_specs=[hbm] + [vmem] * 3 + [hbm] + [vmem] * 2,
        out_specs=vmem,
        scratch_shapes=[
            pltpu.VMEM((traces, toks, feats), bf16),
            pltpu.VMEM((2, traces, block, feats), bf16),
            pltpu.VMEM((traces, block, feats), bf16),
            pltpu.VMEM((traces, block, feats), bf16),
            pltpu.VMEM((traces, block, feats), bf16),
            pltpu.VMEM((2, traces, block, feats), bf16),
            pltpu.VMEM((traces, steps, feats), bf16),
            pltpu.VMEM((chunks, depth, SPAN), bf16),
            pltpu.VMEM((chunks, 2 * depth, SPAN), bf16),
            pltpu.VMEM((mine, steps, SPAN), f32),
            pltpu.VMEM((mine, steps, SPAN), f32),
            pltpu.VMEM((traces, steps, SPAN), f32),
            pltpu.VMEM((traces, steps, SPAN), f32),
            pltpu.VMEM((traces, steps, SPAN), f32),
            pltpu.VMEM((steps, 128), f32),
            pltpu.VMEM((n_dev, traces, steps), f32),
            pltpu.SemaphoreType.REGULAR,
            dma((traces,)), dma((chunks, 2)),
            dma((pieces,)), dma((pieces,)),
            dma((chunks,)), dma((chunks,)),
            dma((pieces,)), dma((pieces,)), dma((pieces,)),
            dma((2 * pieces,)), dma((2 * pieces,)),
            dma((mine,)), dma((mine,)),
            dma((traces,)), dma((traces,)),
            dma((n_dev,)), dma((n_dev,)),
        ],
        compiler_params=pltpu.CompilerParams(collective_id=0, has_side_effects=True),
    )(
        hidden_states, boundary, valid, pairs.T, w_first,
        b_first.reshape(1, width), w_second.reshape(1, width),
    )
    return result[:traces, :steps], result[:traces, steps], result[: pairs.shape[0], steps + 1]


def solution(mesh):
    n_seq, n_head = mesh.shape["seq"], mesh.shape["head"]
    paired = n_seq == 8 and n_head == 4
    body = functools.partial(fused, n_seq, n_head) if paired else per_device
    placed = (P(None, "seq", "head"), P(), P(), P(), P("seq", "head"), P("head"), P("head"))
    return jax.shard_map(
        body, mesh=mesh, in_specs=placed, out_specs=(P(), P(), P()), check_vma=False
    )
```

time: 62.4 us -> 54.4 us (0.87)
  Pallas kernels: 59.1 us -> 51.5 us
    pallas_call x1, Pallas kernels: 59.1 us -> 51.5 us  [fused(): pl.pallas_call(functools.partial(kernel, n_seq, n_head), out_shape=jax.Sh...]
    unnamed x9 -> x3, local copies, waits for them, and re-layouts: 2.38 us -> 0.6 us
    slice x0 -> x1, local copies, waits for them, and re-layouts: none -> 1.51 us  [fused(): result[:pairs.shape[0], steps + 1]]
where the time goes in v1:
time: 54.4 us; the launch traced here: 54.2 us
  Pallas kernels  51.5 us (95%)
  local copies, waits for them, and re-layouts  2.11 us (4%)
  between operations  0.65 us (1%)
    pallas_call x1, Pallas kernels, fused(): pl.pallas_call(functools.partial(kernel, n_seq, n_head), out_shape=jax.Sh...  51.5 us
    slice x1, local copies, waits for them, and re-layouts, fused(): result[:pairs.shape[0], steps + 1]  1.51 us

profile of v1, /device:TPU:0, one launch (start us, length us, event | category | flops | bytes accessed | tf_op | source)
XLA Modules:
  0.0 54.2 jit_solution(3995949170516626325)
XLA Ops:
  0.6 51.5 %shard_map.94 = f32[8,128]{1,0:T(8,128)} custom-call(bf16[8,64,896]{2,1,0:T(8,128)(2,1)} %hid_hbm.1, s32[8,64]{1,0:T(8,128)} %bnd.1, s32[8,64]{1,0:T(8,128)} %valid.1, s32[2,8]{1,0:T(2,128)} %bitcast.7, bf16[448,1024]{1,0:T(8,128)(2,1)} %w_hbm.1, f32[1,1024]{1,0:T(1,128)} %bitcast.5, f32[1,1024]{1,0:T(1,128)} %bitcast.6), custom_call_target="tpu_custom_call" | custom-call | tf_op jit(solution)/shard_map/pallas_call | solution.py:446
  52.1 0.0 copy-start
  52.1 1.5 %slice_reduce_fusion = (f32[8]{0:T(128)}, f32[8]{0:T(128)}) fusion(f32[8,128]{1,0:T(8,128)} %shard_map.94), kind=kLoop, calls=%fused_computation | loop fusion | bytes 128 | tf_op jit(solution)/shard_map/slice | solution.py:483
  53.6 0.0 copy-done
  53.6 0.6 %copy.11 = f32[8,64]{1,0:T(8,128)} copy(f32[8,64]{1,0:T(8,128)S(1)} %bitcast.4) | data formatting | bytes 4096
Async XLA Ops:
  52.1 1.5 %copy-start = (f32[8,128]{1,0:T(8,128)S(1)}, f32[8,128]{1,0:T(8,128)}, u32[]{:S(2)}) copy-start(f32[8,128]{1,0:T(8,128)} %shard_map.94) | copy-start | bytes 12292

commit v2 on v1

--- a/solution.py
+++ b/solution.py
@@ -11,37 +11,42 @@
 SPAN = 128
 HUB_FIRST = 0
 EARLY = 1
-W_MEMBER = (-8, -6, -4, -1)
+W_MEMBER = (-8, 7, 7, 7)
 W_OUTER = (-8, 7, 7, 7)
 W_MIDDLE = (-8, -6, -4, -1)
-PARTS = 1
-AHEAD = 1
-LAG_Y = 8
-LAG_Z = 16
-
-
-def schedule(blocks, chunks):
-    order = [(k, c) for k in range(blocks) for c in range(chunks)]
-    left = {k: chunks for k in range(blocks)}
-    ops, pending, got = [], [], 0
-    for i in range(len(order) + LAG_Y):
+PARTS = 2
+END_LAG = 8
+MID_LAG = 12
+END_AHEAD = 2
+MID_AHEAD = 1
+ROW_PACE = 1.3
+COLUMN_AT = (0, 5.5, 9, 10)
+
+
+def row_order(blocks, chunks):
+    return [(k, c) for k in range(blocks) for c in range(chunks)]
+
+
+def wave_order(blocks, chunks):
+    when = lambda k, c: (max(ROW_PACE * k, COLUMN_AT[c]), c, k)
+    return sorted(row_order(blocks, chunks), key=lambda tile: when(*tile))
+
+
+def schedule(order, blocks, lag, ahead):
+    ops, got, held = [], 0, 0
+    for i in range(len(order) + lag):
         if i < len(order):
             k, c = order[i]
-            while got < min(blocks, k + 1 + AHEAD):
+            while got < min(blocks, k + 1 + ahead):
                 ops.append((0, got, 0))
                 got += 1
-            if c == 0:
-                ops.append((1, k, 0))
+            while held < k + 1:
+                ops.append((1, held, 0))
+                held += 1
             ops.append((2, k, c))
-        if i >= LAG_Y:
-            k, c = order[i - LAG_Y]
-            ops.append((3, k, c))
-            left[k] -= 1
-            if left[k] == 0:
-                pending.append((i + LAG_Z, k))
-        while pending and pending[0][0] <= i:
-            ops.append((4, pending.pop(0)[1], 0))
-    return ops + [(4, k, 0) for _, k in pending]
+        if i >= lag:
+            ops.append((3, *order[i - lag]))
+    return ops
 
 
 def score_rows(rows, w_first, b_first, w_second):
@@ -75,7 +80,7 @@
 def kernel(
     n_seq, n_head, hid_hbm, bnd, valid, pairs, w_hbm, b, w2, result,
     hid, xo, xin, xup, xdn, xq, xl, wown, wall,
-    ysend, yrecv, zsend, zrecv, kept, fsend, frecv, far,
+    ysend, yrecv, zsend, zrecv, kept, whole, fsend, frecv, far,
     s_hid, s_win, s_x1, r_x1, s_w, r_w, s_x2, r_up, r_dn, s_x3, r_x3,
     s_y, r_y, s_z, r_z, s_f, r_f,
 ):
@@ -270,26 +275,22 @@
         copy_x3(par, n, 1).start()
         copy_x3(par, n, 0).start()
 
-    def collect(n):
-        k, rows = n // PARTS, rows_of(n)
-        if k >= HUB_FIRST:
-
-            @pl.when(hub)
-            def _():
+    def collect(n, ends):
+        k, rows = n // PARTS, rows_of(n)
+
+        @pl.when(member)
+        def _():
+            if ends:
+                copy_up(n).wait_recv()
+                xq[par, k, rows] = xo[y, k, rows] + xup[k, rows]
+                copy_x3(par, n, 1).start()
+                copy_x3(par, n, 0).start()
+            elif k >= HUB_FIRST:
                 gather(n)
 
-        @pl.when(member & is_end)
-        def _():
-            copy_up(n).wait_recv()
-            xq[par, k, rows] = xo[y, k, rows] + xup[k, rows]
-            copy_x3(par, n, 1).start()
-
         @pl.when(jnp.logical_not(member))
         def _():
             copy_x3(par, n, 1).wait_recv()
-
-        @pl.when(jnp.logical_not(hub))
-        def _():
             copy_x3(par, n, 0).start()
 
     def ready(k):
@@ -328,7 +329,7 @@
     def give(k, c):
         t = k * (chunks // 2) + c // 2
 
-        @pl.when(c % 2 != y)
+        @pl.when(y != (c + k) % 2)
         def _():
             ysend[t] = part(k, c)
             copy_y(t).start()
@@ -336,45 +337,54 @@
     def take(k, c):
         t = k * (chunks // 2) + c // 2
 
-        @pl.when((c % 2 == y) & (c // 2 != high))
-        def _():
-            zsend[k] = part(k, c)
+        @pl.when(y == (c + k) % 2)
+        def _():
+            kept[t] = part(k, c)
             copy_y(t).wait_recv()
-            zsend[k] = zsend[k] + yrecv[t]
-            copy_z(k).start()
-
-        @pl.when((c % 2 == y) & (c // 2 == high))
-        def _():
-            kept[k] = part(k, c)
-            copy_y(t).wait_recv()
-            kept[k] = kept[k] + yrecv[t]
-
-    at = pl.ds(pl.multiple_of((odd * chunks + 2 * high + y) * span, span), span)
-    bias = b[:, at]
-    out_row = w2[:, at]
+
+            @pl.when(high != (c // 2 + k // 2) % 2)
+            def _():
+                zsend[k] = kept[t] + yrecv[t]
+                copy_z(k).start()
+
+            @pl.when(high == (c // 2 + k // 2) % 2)
+            def _():
+                whole[k] = kept[t] + yrecv[t]
 
     def finish(k):
+        c = 2 * lax.rem(high + k // 2, 2) + lax.rem(y + k, 2)
+        at = pl.ds(pl.multiple_of((odd * chunks + c) * span, span), span)
         copy_z(k).wait_recv()
-        act = jnp.maximum(kept[k] + zrecv[k] + bias, 0.0) * out_row
+        act = jnp.maximum(whole[k] + zrecv[k] + b[:, at], 0.0) * w2[:, at]
         total = jnp.sum(act, axis=1, keepdims=True)
         fsend[...] = fsend[...] + jnp.where(spots == trace_of(k), total, 0.0)
 
     pl.semaphore_wait(far, 1)
-    arrived = set()
-    for kind, k, c in schedule(blocks, chunks):
-        if kind == 0:
-            for p in range(PARTS):
-                collect(k * PARTS + p)
-        elif kind == 1:
-            ready(k)
-        elif kind == 4:
-            finish(k)
-        else:
-            if c not in arrived:
-                arrived.add(c)
-                fetch_w(c, True).wait()
-                copy_w(c).wait_recv()
-            (give if kind == 2 else take)(k, c)
+    def run(order, lag, ahead, ends):
+        arrived = set()
+        for kind, k, c in schedule(order, blocks, lag, ahead):
+            if kind == 0:
+                for p in range(PARTS):
+                    collect(k * PARTS + p, ends)
+            elif kind == 1:
+                ready(k)
+            else:
+                if c not in arrived:
+                    arrived.add(c)
+                    fetch_w(c, True).wait()
+                    copy_w(c).wait_recv()
+                (give if kind == 2 else take)(k, c)
+
+    @pl.when(is_end)
+    def _():
+        run(row_order(blocks, chunks), END_LAG, END_AHEAD, True)
+
+    @pl.when(middle)
+    def _():
+        run(wave_order(blocks, chunks), MID_LAG, MID_AHEAD, False)
+
+    for k in range(blocks):
+        finish(k)
 
     me = s * n_head + h
     n_dev = n_seq * n_head
@@ -388,6 +398,21 @@
     frecv[me] = jnp.transpose(fsend[...])[: frecv.shape[1], :]
     for d in range(1, n_dev):
         copy_f(d).start()
+    for c in range(chunks):
+        copy_w(c).wait_send()
+    for n in range(pieces):
+        copy_x1(n).wait_send()
+        copy_up(n).wait_send()
+        copy_x3(par, n, 0).wait_send()
+
+        @pl.when(member)
+        def _():
+            copy_x3(par, n, 1).wait_send()
+
+    for t in range(blocks * chunks // 2):
+        copy_y(t).wait_send()
+    for k in range(blocks):
+        copy_z(k).wait_send()
     for i in range(n_dev):
 
         @pl.when(me != i)
@@ -411,21 +436,6 @@
     result[:traces, steps : steps + 1] = low
     result[: pairs.shape[1], steps + 1 : steps + 2] = gap
 
-    for c in range(chunks):
-        copy_w(c).wait_send()
-    for n in range(pieces):
-        copy_x1(n).wait_send()
-        copy_up(n).wait_send()
-        copy_x3(par, n, 0).wait_send()
-
-        @pl.when(member)
-        def _():
-            copy_x3(par, n, 1).wait_send()
-
-    for t in range(blocks * chunks // 2):
-        copy_y(t).wait_send()
-    for k in range(blocks):
-        copy_z(k).wait_send()
     for d in range(1, n_dev):
         copy_f(d).wait_send()
 
@@ -462,6 +472,7 @@
             pltpu.VMEM((mine, steps, SPAN), f32),
             pltpu.VMEM((traces, steps, SPAN), f32),
             pltpu.VMEM((traces, steps, SPAN), f32),
+            pltpu.VMEM((mine, steps, SPAN), f32),
             pltpu.VMEM((traces, steps, SPAN), f32),
             pltpu.VMEM((steps, 128), f32),
             pltpu.VMEM((n_dev, traces, steps), f32),

time: 54.4 us -> 52.3 us (0.961)
  Pallas kernels: 51.5 us -> 49.3 us
    pallas_call x1, Pallas kernels: 51.5 us -> 49.3 us  [fused(): pl.pallas_call(functools.partial(kernel, n_seq, n_head), out_shape=jax.Sh...]
where the time goes in v2:
time: 52.3 us; the launch traced here: 52.1 us
  Pallas kernels  49.3 us (94%)
  local copies, waits for them, and re-layouts  2.11 us (4%)
  between operations  0.65 us (1%)
    pallas_call x1, Pallas kernels, fused(): pl.pallas_call(functools.partial(kernel, n_seq, n_head), out_shape=jax.Sh...  49.3 us
    slice x1, local copies, waits for them, and re-layouts, fused(): result[:pairs.shape[0], steps + 1]  1.51 us

profile of v2, /device:TPU:0, one launch (start us, length us, event | category | flops | bytes accessed | tf_op | source)
XLA Modules:
  0.0 52.1 jit_solution(8589712189706926093)
XLA Ops:
  0.6 49.3 %shard_map.94 = f32[8,128]{1,0:T(8,128)} custom-call(bf16[8,64,896]{2,1,0:T(8,128)(2,1)} %hid_hbm.1, s32[8,64]{1,0:T(8,128)} %bnd.1, s32[8,64]{1,0:T(8,128)} %valid.1, s32[2,8]{1,0:T(2,128)} %bitcast.7, bf16[448,1024]{1,0:T(8,128)(2,1)} %w_hbm.1, f32[1,1024]{1,0:T(1,128)} %bitcast.5, f32[1,1024]{1,0:T(1,128)} %bitcast.6), custom_call_target="tpu_custom_call" | custom-call | tf_op jit(solution)/shard_map/pallas_call | solution.py:456
  49.9 0.0 copy-start
  49.9 1.5 %slice_reduce_fusion = (f32[8]{0:T(128)}, f32[8]{0:T(128)}) fusion(f32[8,128]{1,0:T(8,128)} %shard_map.94), kind=kLoop, calls=%fused_computation | loop fusion | bytes 128 | tf_op jit(solution)/shard_map/slice | solution.py:494
  51.5 0.0 copy-done
  51.5 0.6 %copy.11 = f32[8,64]{1,0:T(8,128)} copy(f32[8,64]{1,0:T(8,128)S(1)} %bitcast.4) | data formatting | bytes 4096
Async XLA Ops:
  49.9 1.5 %copy-start = (f32[8,128]{1,0:T(8,128)S(1)}, f32[8,128]{1,0:T(8,128)}, u32[]{:S(2)}) copy-start(f32[8,128]{1,0:T(8,128)} %shard_map.94) | copy-start | bytes 12292

commit v3 on v2

--- a/solution.py
+++ b/solution.py
@@ -15,6 +15,8 @@
 W_OUTER = (-8, 7, 7, 7)
 W_MIDDLE = (-8, -6, -4, -1)
 PARTS = 2
+LEAN_A = (6, 7)
+LEAN_B = (7,)
 END_LAG = 8
 MID_LAG = 12
 END_AHEAD = 2
@@ -80,7 +82,7 @@
 def kernel(
     n_seq, n_head, hid_hbm, bnd, valid, pairs, w_hbm, b, w2, result,
     hid, xo, xin, xup, xdn, xq, xl, wown, wall,
-    ysend, yrecv, zsend, zrecv, kept, whole, fsend, frecv, far,
+    ysend, yrecv, zsend, zrecv, kept, fsend, frecv, far,
     s_hid, s_win, s_x1, r_x1, s_w, r_w, s_x2, r_up, r_dn, s_x3, r_x3,
     s_y, r_y, s_z, r_z, s_f, r_f,
 ):
@@ -186,12 +188,12 @@
     def copy_x1(n):
         k, rows = n // PARTS, rows_of(n)
         return remote(
-            xo.at[other, k, rows], xin.at[k, rows], s_x1.at[n], r_x1.at[n], across, h
+            xo.at[other, k, rows], xin.at[k, rows], s_x1, r_x1.at[n], across, h
         )
 
     def copy_w(c):
         rows = pl.ds(pl.multiple_of(odd * depth, depth), depth)
-        return remote(wown.at[c], wall.at[c, rows, :], s_w.at[c], r_w.at[c], s_near, h)
+        return remote(wown.at[c], wall.at[c, rows, :], s_w, r_w.at[c], s_near, h)
 
     for k in range(EARLY):
         pick(k)
@@ -230,19 +232,19 @@
         k, rows = n // PARTS, rows_of(n)
         to_s = jnp.where(member, s_near, jnp.where(h >= n_head // 2, s + 2, s - 2))
         return remote(
-            xo.at[y, k, rows], xup.at[k, rows], s_x2.at[n], r_up.at[n],
+            xo.at[y, k, rows], xup.at[k, rows], s_x2, r_up.at[n],
             lax.rem(to_s + n_seq, n_seq), h,
         )
 
     def copy_dn(n):
         k, rows = n // PARTS, rows_of(n)
-        return remote(xo.at[y, k, rows], xdn.at[k, rows], s_x2.at[n], r_dn.at[n], s_near, h)
+        return remote(xo.at[y, k, rows], xdn.at[k, rows], s_x2, r_dn.at[n], s_near, h)
 
     def copy_x3(q, n, way):
         k, rows = n // PARTS, rows_of(n)
         to_h = h_x if way else h_core
         return remote(
-            xq.at[q, k, rows], xq.at[q, k, rows], s_x3.at[way * pieces + n],
+            xq.at[q, k, rows], xq.at[q, k, rows], s_x3.at[way],
             r_x3.at[q * pieces + n], s, to_h,
         )
 
@@ -315,10 +317,10 @@
             gather(n)
 
     def copy_y(t):
-        return remote(ysend.at[t], yrecv.at[t], s_y.at[t], r_y.at[t], across, h)
+        return remote(ysend.at[t], yrecv.at[t], s_y, r_y.at[t], across, h)
 
     def copy_z(t):
-        return remote(zsend.at[t], zrecv.at[t], s_z.at[t], r_z.at[t], s_far, h)
+        return remote(zsend.at[t], zrecv.at[t], s_z, r_z.at[t], s_far, h)
 
     spots = lax.broadcasted_iota(jnp.int32, (steps, 128), 1)
     fsend[...] = jnp.zeros_like(fsend)
@@ -326,6 +328,13 @@
     def part(k, c):
         return jnp.dot(xl[k], wall[c], preferred_element_type=jnp.float32)
 
+    def owner_of(k, j):
+        base = (j + k // 2) % 2
+        return (1 if k in LEAN_A else base, 0 if k in LEAN_B else base)
+
+    def owner(k, j):
+        return jnp.where(h < n_head // 2, *owner_of(k, j))
+
     def give(k, c):
         t = k * (chunks // 2) + c // 2
 
@@ -342,22 +351,26 @@
             kept[t] = part(k, c)
             copy_y(t).wait_recv()
 
-            @pl.when(high != (c // 2 + k // 2) % 2)
+            @pl.when(high != owner(k, c // 2))
             def _():
-                zsend[k] = kept[t] + yrecv[t]
-                copy_z(k).start()
-
-            @pl.when(high == (c // 2 + k // 2) % 2)
+                zsend[t] = kept[t] + yrecv[t]
+                copy_z(t).start()
+
+            @pl.when(high == owner(k, c // 2))
             def _():
-                whole[k] = kept[t] + yrecv[t]
-
-    def finish(k):
-        c = 2 * lax.rem(high + k // 2, 2) + lax.rem(y + k, 2)
-        at = pl.ds(pl.multiple_of((odd * chunks + c) * span, span), span)
-        copy_z(k).wait_recv()
-        act = jnp.maximum(whole[k] + zrecv[k] + b[:, at], 0.0) * w2[:, at]
-        total = jnp.sum(act, axis=1, keepdims=True)
-        fsend[...] = fsend[...] + jnp.where(spots == trace_of(k), total, 0.0)
+                kept[t] = kept[t] + yrecv[t]
+
+    def finish(k, j):
+        c = 2 * j + lax.rem(y + k, 2)
+        t = k * (chunks // 2) + j
+
+        @pl.when(high == owner(k, j))
+        def _():
+            at = pl.ds(pl.multiple_of((odd * chunks + c) * span, span), span)
+            copy_z(t).wait_recv()
+            act = jnp.maximum(kept[t] + zrecv[t] + b[:, at], 0.0) * w2[:, at]
+            total = jnp.sum(act, axis=1, keepdims=True)
+            fsend[...] = fsend[...] + jnp.where(spots == trace_of(k), total, 0.0)
 
     pl.semaphore_wait(far, 1)
     def run(order, lag, ahead, ends):
@@ -384,7 +397,8 @@
         run(wave_order(blocks, chunks), MID_LAG, MID_AHEAD, False)
 
     for k in range(blocks):
-        finish(k)
+        for j in range(chunks // 2):
+            finish(k, j)
 
     me = s * n_head + h
     n_dev = n_seq * n_head
@@ -392,32 +406,38 @@
     def copy_f(d):
         to = lax.rem(me + d, n_dev)
         return remote(
-            frecv.at[me], frecv.at[me], s_f.at[d], r_f.at[me], to // n_head, lax.rem(to, n_head)
+            frecv.at[me], frecv.at[me], s_f, r_f, to // n_head, lax.rem(to, n_head)
         )
 
     frecv[me] = jnp.transpose(fsend[...])[: frecv.shape[1], :]
     for d in range(1, n_dev):
         copy_f(d).start()
-    for c in range(chunks):
-        copy_w(c).wait_send()
-    for n in range(pieces):
-        copy_x1(n).wait_send()
-        copy_up(n).wait_send()
-        copy_x3(par, n, 0).wait_send()
-
-        @pl.when(member)
-        def _():
-            copy_x3(par, n, 1).wait_send()
-
-    for t in range(blocks * chunks // 2):
-        copy_y(t).wait_send()
-    for k in range(blocks):
-        copy_z(k).wait_send()
-    for i in range(n_dev):
-
-        @pl.when(me != i)
-        def _():
-            remote(frecv.at[i], frecv.at[i], s_f.at[0], r_f.at[i], across, h).wait_recv()
+    def drain(ref, sem):
+        remote(ref, ref, sem, r_f, across, h).wait_send()
+
+    drain(wown, s_w)
+    drain(xin, s_x1)
+    drain(xin, s_x2)
+    drain(xin, s_x3.at[0])
+
+    @pl.when(member)
+    def _():
+        drain(xin, s_x3.at[1])
+
+    drain(ysend, s_y)
+    left = h < n_head // 2
+    for side in range(2):
+        for up in range(2):
+            sent = sum(
+                up != owner_of(k, j)[side] for k in range(blocks) for j in range(chunks // 2)
+            )
+
+            @pl.when((left == (side == 0)) & (high == up))
+            def _():
+                drain(zsend.at[pl.ds(0, sent)], s_z)
+
+    others = frecv.at[pl.ds(0, n_dev - 1)]
+    remote(others, others, s_f, r_f, across, h).wait_recv()
 
     sums = [frecv[i] for i in range(4)]
     for i in range(4, n_dev):
@@ -436,8 +456,7 @@
     result[:traces, steps : steps + 1] = low
     result[: pairs.shape[1], steps + 1 : steps + 2] = gap
 
-    for d in range(1, n_dev):
-        copy_f(d).wait_send()
+    drain(others, s_f)
 
 
 def fused(n_seq, n_head, hidden_states, boundary, valid, pairs, w_first, b_first, w_second):
@@ -470,21 +489,20 @@
             pltpu.VMEM((chunks, 2 * depth, SPAN), bf16),
             pltpu.VMEM((mine, steps, SPAN), f32),
             pltpu.VMEM((mine, steps, SPAN), f32),
-            pltpu.VMEM((traces, steps, SPAN), f32),
-            pltpu.VMEM((traces, steps, SPAN), f32),
             pltpu.VMEM((mine, steps, SPAN), f32),
-            pltpu.VMEM((traces, steps, SPAN), f32),
+            pltpu.VMEM((mine, steps, SPAN), f32),
+            pltpu.VMEM((mine, steps, SPAN), f32),
             pltpu.VMEM((steps, 128), f32),
             pltpu.VMEM((n_dev, traces, steps), f32),
             pltpu.SemaphoreType.REGULAR,
             dma((traces,)), dma((chunks, 2)),
-            dma((pieces,)), dma((pieces,)),
-            dma((chunks,)), dma((chunks,)),
-            dma((pieces,)), dma((pieces,)), dma((pieces,)),
-            dma((2 * pieces,)), dma((2 * pieces,)),
-            dma((mine,)), dma((mine,)),
-            dma((traces,)), dma((traces,)),
-            dma((n_dev,)), dma((n_dev,)),
+            dma, dma((pieces,)),
+            dma, dma((chunks,)),
+            dma, dma((pieces,)), dma((pieces,)),
+            dma((2,)), dma((2 * pieces,)),
+            dma, dma((mine,)),
+            dma, dma((mine,)),
+            dma, dma,
         ],
         compiler_params=pltpu.CompilerParams(collective_id=0, has_side_effects=True),
     )(

time: 52.3 us -> 50.5 us (0.966)
  Pallas kernels: 49.3 us -> 47.6 us
    pallas_call x1, Pallas kernels: 49.3 us -> 47.6 us  [fused(): pl.pallas_call(functools.partial(kernel, n_seq, n_head), out_shape=jax.Sh...]
where the time goes in v3:
time: 50.5 us; the launch traced here: 50.3 us
  Pallas kernels  47.6 us (94%)
  local copies, waits for them, and re-layouts  2.11 us (4%)
  between operations  0.65 us (1%)
    pallas_call x1, Pallas kernels, fused(): pl.pallas_call(functools.partial(kernel, n_seq, n_head), out_shape=jax.Sh...  47.6 us
    slice x1, local copies, waits for them, and re-layouts, fused(): result[:pairs.shape[0], steps + 1]  1.51 us

profile of v3, /device:TPU:0, one launch (start us, length us, event | category | flops | bytes accessed | tf_op | source)
XLA Modules:
  0.0 50.3 jit_solution(17149066697147210571)
XLA Ops:
  0.6 47.6 %shard_map.94 = f32[8,128]{1,0:T(8,128)} custom-call(bf16[8,64,896]{2,1,0:T(8,128)(2,1)} %hid_hbm.1, s32[8,64]{1,0:T(8,128)} %bnd.1, s32[8,64]{1,0:T(8,128)} %valid.1, s32[2,8]{1,0:T(2,128)} %bitcast.7, bf16[448,1024]{1,0:T(8,128)(2,1)} %w_hbm.1, f32[1,1024]{1,0:T(1,128)} %bitcast.5, f32[1,1024]{1,0:T(1,128)} %bitcast.6), custom_call_target="tpu_custom_call" | custom-call | tf_op jit(solution)/shard_map/pallas_call | solution.py:475
  48.2 0.0 copy-start
  48.2 1.5 %slice_reduce_fusion = (f32[8]{0:T(128)}, f32[8]{0:T(128)}) fusion(f32[8,128]{1,0:T(8,128)} %shard_map.94), kind=kLoop, calls=%fused_computation | loop fusion | bytes 128 | tf_op jit(solution)/shard_map/slice | solution.py:512
  49.7 0.0 copy-done
  49.7 0.6 %copy.11 = f32[8,64]{1,0:T(8,128)} copy(f32[8,64]{1,0:T(8,128)S(1)} %bitcast.4) | data formatting | bytes 4096
Async XLA Ops:
  48.2 1.5 %copy-start = (f32[8,128]{1,0:T(8,128)S(1)}, f32[8,128]{1,0:T(8,128)}, u32[]{:S(2)}) copy-start(f32[8,128]{1,0:T(8,128)} %shard_map.94) | copy-start | bytes 12292

commit v4 on v3

--- a/solution.py
+++ b/solution.py
@@ -9,7 +9,7 @@
 
 MESH = pl.DeviceIdType.MESH
 SPAN = 128
-HUB_FIRST = 0
+HUB_FIRST = 4
 EARLY = 1
 W_MEMBER = (-8, 7, 7, 7)
 W_OUTER = (-8, 7, 7, 7)
@@ -110,7 +110,7 @@
         return pltpu.make_async_copy(
             w_hbm.at[:, pl.ds(first, span)],
             wall.at[c, rows, :] if mine else wown.at[c],
-            s_win.at[c, 1 if mine else 0],
+            s_win.at[chunks if mine else c],
         )
 
     def trace_of(k):
@@ -245,7 +245,7 @@
         to_h = h_x if way else h_core
         return remote(
             xq.at[q, k, rows], xq.at[q, k, rows], s_x3.at[way],
-            r_x3.at[q * pieces + n], s, to_h,
+            r_x3.at[n if way else pieces + k], s, to_h,
         )
 
     def relay(n):
@@ -296,8 +296,8 @@
             copy_x3(par, n, 0).start()
 
     def ready(k):
-        for p in range(PARTS):
-            copy_x3(1 - par, k * PARTS + p, 0).wait_recv()
+        both = xq.at[1 - par, k]
+        remote(both, both, s_x3.at[0], r_x3.at[pieces + k], s, h_core).wait_recv()
         low = xq[0, k].astype(jnp.float32)
         top = xq[1, k].astype(jnp.float32)
         pair = fold(low, top)
@@ -373,6 +373,8 @@
             fsend[...] = fsend[...] + jnp.where(spots == trace_of(k), total, 0.0)
 
     pl.semaphore_wait(far, 1)
+    pltpu.make_async_copy(wown, wown, s_win.at[chunks]).wait()
+
     def run(order, lag, ahead, ends):
         arrived = set()
         for kind, k, c in schedule(order, blocks, lag, ahead):
@@ -384,7 +386,6 @@
             else:
                 if c not in arrived:
                     arrived.add(c)
-                    fetch_w(c, True).wait()
                     copy_w(c).wait_recv()
                 (give if kind == 2 else take)(k, c)
 
@@ -495,11 +496,11 @@
             pltpu.VMEM((steps, 128), f32),
             pltpu.VMEM((n_dev, traces, steps), f32),
             pltpu.SemaphoreType.REGULAR,
-            dma((traces,)), dma((chunks, 2)),
+            dma((traces,)), dma((chunks + 1,)),
             dma, dma((pieces,)),
             dma, dma((chunks,)),
             dma, dma((pieces,)), dma((pieces,)),
-            dma((2,)), dma((2 * pieces,)),
+            dma((2,)), dma((pieces + traces,)),
             dma, dma((mine,)),
             dma, dma((mine,)),
             dma, dma,

time: 50.5 us -> 50.4 us (level)
  no operation moved by 1% of the time
where the time goes in v4:
time: 50.4 us; the launch traced here: 50.2 us
  Pallas kernels  47.4 us (94%)
  local copies, waits for them, and re-layouts  2.11 us (4%)
  between operations  0.65 us (1%)
    pallas_call x1, Pallas kernels, fused(): pl.pallas_call(functools.partial(kernel, n_seq, n_head), out_shape=jax.Sh...  47.4 us
    slice x1, local copies, waits for them, and re-layouts, fused(): result[:pairs.shape[0], steps + 1]  1.51 us

profile of v4, /device:TPU:0, one launch (start us, length us, event | category | flops | bytes accessed | tf_op | source)
XLA Modules:
  0.0 50.2 jit_solution(14236008228569499568)
XLA Ops:
  0.6 47.4 %shard_map.94 = f32[8,128]{1,0:T(8,128)} custom-call(bf16[8,64,896]{2,1,0:T(8,128)(2,1)} %hid_hbm.1, s32[8,64]{1,0:T(8,128)} %bnd.1, s32[8,64]{1,0:T(8,128)} %valid.1, s32[2,8]{1,0:T(2,128)} %bitcast.7, bf16[448,1024]{1,0:T(8,128)(2,1)} %w_hbm.1, f32[1,1024]{1,0:T(1,128)} %bitcast.5, f32[1,1024]{1,0:T(1,128)} %bitcast.6), custom_call_target="tpu_custom_call" | custom-call | tf_op jit(solution)/shard_map/pallas_call | solution.py:476
  48.1 0.0 copy-start
  48.1 1.5 %slice_reduce_fusion = (f32[8]{0:T(128)}, f32[8]{0:T(128)}) fusion(f32[8,128]{1,0:T(8,128)} %shard_map.94), kind=kLoop, calls=%fused_computation | loop fusion | bytes 128 | tf_op jit(solution)/shard_map/slice | solution.py:513
  49.6 0.0 copy-done
  49.6 0.6 %copy.11 = f32[8,64]{1,0:T(8,128)} copy(f32[8,64]{1,0:T(8,128)S(1)} %bitcast.4) | data formatting | bytes 4096
Async XLA Ops:
  48.1 1.5 %copy-start = (f32[8,128]{1,0:T(8,128)S(1)}, f32[8,128]{1,0:T(8,128)}, u32[]{:S(2)}) copy-start(f32[8,128]{1,0:T(8,128)} %shard_map.94) | copy-start | bytes 12292
